TPU v7x, 32 devices: a whole 2x2x4 slice. The times are simulated.
32 devices in a mesh: grid: 2 (over x), prow: 4 (over y, core), pcol: 4 (over z).
Axes of the slice: x: 2, y: 2, z: 4, core: 2. Of those that a mesh axis runs over, the one named last changes fastest.
Arguments:
- sub_rhs: float32 [2, 3, 64, 3072], P('grid', None, None, 'prow'), may hold values from -6 to 6
- root_rhs: float32 [64, 3072], P(None, 'prow'), may hold values from -6 to 6
- diag_inverse: bfloat16 [3, 3072, 6144], P(None, 'prow', ('grid', 'pcol'))
- root_inverse: bfloat16 [3072, 3072], P('prow', 'grid')
- inner_factor: bfloat16 [3, 6144, 3072], P(None, ('grid', 'pcol'), 'prow'), may hold values from -0.078125 to 0.078125
- inner_mask: int32 [3, 48, 24], P(None, ('grid', 'pcol')), may hold values 0 or 1
- root_factor: bfloat16 [3, 6144, 3072], P(None, ('grid', 'pcol'), 'prow'), may hold values from -0.078125 to 0.078125
- root_mask: int32 [3, 48, 24], P(None, ('grid', 'pcol')), may hold values 0 or 1
Outputs:
- sub_solution: float32 [3, 64, 6144], P(None, None, ('grid', 'pcol'))
- root_solution: float32 [64, 3072], P(None, 'grid')
Inputs may be any that keep to these rules, and one draw needn't show every extreme that they name: `inner_mask`: 1 keeps a tile of 128 x 128 entries, 0 makes it zero. `root_mask`: 1 keeps a tile of 128 x 128 entries, 0 makes it zero.
All inputs are finite; a program needn't handle non-finite values. No bound on the sum of `inner_mask` or of `root_mask` on one device may be relied on, other than what follows from the above.
Results may differ from a plain program's by a relative error of at most 0.0065.
Values sent between devices are 32-bit elements; how exact they have to be, the bound alone decides.
A program may use at most 64 MiB of HBM per device.

v0:
```python
import jax
import jax.numpy as jnp
from jax import lax
from jax.sharding import PartitionSpec as P

NS = 3072
LEVELS = 3
TILE = 128


def from_partner(shard, axis, bit):
    return lax.ppermute(shard, axis, [(i, i ^ 1 << bit) for i in range(lax.axis_size(axis))])


def selector(positions, count):
    return (positions[:, None] // TILE == jnp.arange(count)[None, :]).astype(jnp.float32)


def masked(factor, mask, row_select, col_select):
    expanded = jnp.dot(jnp.dot(row_select, mask.astype(jnp.float32)), col_select.T)
    return factor * expanded.astype(jnp.bfloat16)


def solve_block(residual, inverse):
    partial_sum = jnp.dot(
        residual.astype(jnp.bfloat16), inverse, preferred_element_type=jnp.float32
    )
    return lax.psum(partial_sum, "prow")


def group_sum(partial_sum, owners):
    summed = partial_sum
    for bit_number in range(owners.bit_length() - 1):
        summed = summed + from_partner(summed, "pcol", bit_number)
    return summed


def shards(
    sub_rhs, root_rhs, diag_inverse, root_inverse, inner_factor, inner_mask, root_factor, root_mask
):
    rows_here = inner_factor.shape[1]
    out_cols = inner_factor.shape[2]
    owners = NS // rows_here
    own_tree = lax.axis_index("pcol") // owners
    col_positions = lax.axis_index("prow") * out_cols + jnp.arange(out_cols)
    row_select = selector(jnp.arange(rows_here), inner_mask.shape[1])
    col_select = selector(col_positions, inner_mask.shape[2])
    own_rhs = lax.dynamic_index_in_dim(sub_rhs, own_tree, 0, keepdims=False)
    kept = []
    solved_all = []
    pair = 0
    for level in range(LEVELS):
        residual = own_rhs[level]
        if level > 0:
            local_update = jnp.zeros(residual.shape, jnp.float32)
            for source in range(level):
                factor_tile = masked(inner_factor[pair], inner_mask[pair], row_select, col_select)
                local_update = local_update + jnp.dot(
                    kept[source], factor_tile, preferred_element_type=jnp.float32
                )
                pair += 1
            residual = residual - group_sum(local_update, owners)
        solved = solve_block(residual, diag_inverse[level])
        solved_all.append(solved)
        kept.append(solved.astype(jnp.bfloat16))
    root_local = jnp.zeros(root_rhs.shape, jnp.float32)
    for source in range(LEVELS):
        factor_tile = masked(root_factor[source], root_mask[source], row_select, col_select)
        root_local = root_local + jnp.dot(
            kept[source], factor_tile, preferred_element_type=jnp.float32
        )
    across = lax.psum(root_local, "pcol")
    root_update = lax.psum(across, "grid")
    root_solution = solve_block(root_rhs - root_update, root_inverse)
    return (jnp.stack(solved_all), root_solution)


def solution(mesh):
    return jax.shard_map(
        shards,
        mesh=mesh,
        in_specs=(
            P("grid", None, None, "prow"),
            P(None, "prow"),
            P(None, "prow", ("grid", "pcol")),
            P("prow", "grid"),
            P(None, ("grid", "pcol"), "prow"),
            P(None, ("grid", "pcol"), None),
            P(None, ("grid", "pcol"), "prow"),
            P(None, ("grid", "pcol"), None),
        ),
        out_specs=(P(None, None, ("grid", "pcol")), P(None, "grid")),
        check_vma=False,
    )
```

profile of v0, /device:TPU:0, one launch (start us, length us, event | category | flops | bytes accessed | tf_op | source)
XLA Modules:
  0.0 262.5 jit_solution(7148002226130458398)
XLA Ops:
  7.2 0.0 copy-start
  7.2 0.0 all-reduce.7.cloned.1.call-start
  7.2 2.5 fusion.22
  9.8 0.0 all-reduce.7.cloned.1.call-update
  9.8 0.0 all-reduce.9.cloned.1.call-start
  9.9 0.3 fusion.41
  10.2 0.3 fusion.39
  10.4 0.6 add_select_fusion
  11.0 34.6 %all-reduce.7.cloned.1.call-done = f32[64,768]{1,0:T(8,128)} async-done(((f32[64,768]{1,0:T(8,128)}), f32[64,768]{1,0:T(8,128)}) %all-reduce.7.cloned.1.call-update) | async-done | bytes 196624 | tf_op jit(solution)/shard_map/psum | solution.py:28
  45.7 2.1 fusion.11
  47.8 1.6 collective-permute-start
  49.4 1.0 fusion.40
  50.3 3.2 %collective-permute-done = f32[64,768]{1,0:T(8,128)S(1)} collective-permute-done((f32[64,768]{1,0:T(8,128)S(1)}, f32[64,768]{1,0:T(8,128)S(1)}, u32[]{:S(2)}, u32[]{:S(2)}) %collective-permute-start) | collective-permute-done | bytes 196640 | tf_op jit(solution)/shard_map/ppermute | solution.py:12
  53.6 2.5 collective-permute-start.1
  56.0 1.7 fusion.37
  57.7 5.2 %collective-permute-done.1 = f32[64,768]{1,0:T(8,128)S(1)} collective-permute-done((f32[64,768]{1,0:T(8,128)S(1)}, f32[64,768]{1,0:T(8,128)S(1)}, u32[]{:S(2)}, u32[]{:S(2)}) %collective-permute-start.1) | collective-permute-done | bytes 196640 | tf_op jit(solution)/shard_map/ppermute | solution.py:12
  62.9 2.3 fusion.19
  65.2 0.0 all-reduce.9.cloned.1.call-update
  65.2 0.0 all-reduce.11.cloned.1.call-start
  65.3 1.0 fusion.38
  66.3 32.6 %all-reduce.9.cloned.1.call-done = f32[64,768]{1,0:T(8,128)} async-done(((f32[64,768]{1,0:T(8,128)}), f32[64,768]{1,0:T(8,128)}) %all-reduce.9.cloned.1.call-update) | async-done | bytes 196624 | tf_op jit(solution)/shard_map/psum | solution.py:28
  98.8 2.8 %fusion.9 = f32[64,768]{1,0:T(8,128)} fusion(bf16[768,24]{1,0:T(8,128)(2,1)S(1)} %fusion.39, bf16[3,768,768]{2,1,0:T(8,128)(2,1)} %param.12, s32[768]{0:T(1024)S(1)} %copy-done.10, f32[64,768]{1,0:T(8,128)} %all-reduce.9.cloned.1.call-done), kind=kOutput, calls=%fused_computation.15 | convolution fusion | flops 104466432 | bytes 1612800 | tf_op jit(solution)/shard_map/dot_general | solution.py:58
  101.7 2.2 fusion.33
  103.9 0.0 copy-start.7
  103.9 1.6 collective-permute-start.2
  105.4 1.0 fusion.36
  106.4 3.2 %collective-permute-done.2 = f32[64,768]{1,0:T(8,128)S(1)} collective-permute-done((f32[64,768]{1,0:T(8,128)S(1)}, f32[64,768]{1,0:T(8,128)S(1)}, u32[]{:S(2)}, u32[]{:S(2)}) %collective-permute-start.2) | collective-permute-done | bytes 196640 | tf_op jit(solution)/shard_map/ppermute | solution.py:12
  109.6 1.0 add.63
  110.6 2.5 collective-permute-start.3
  113.0 2.8 %fusion.7 = f32[64,768]{1,0:T(8,128)} fusion(bf16[768,24]{1,0:T(8,128)(2,1)} %fusion.37, bf16[3,768,768]{2,1,0:T(8,128)(2,1)} %param.14, s32[768]{0:T(1024)} %add_select_fusion, f32[64,768]{1,0:T(8,128)S(1)} %copy-done.4), kind=kOutput, calls=%fused_computation.13 | convolution fusion | flops 104466432 | bytes 1773568 | tf_op jit(solution)/shard_map/dot_general | solution.py:69
  115.9 4.1 %collective-permute-done.3 = f32[64,768]{1,0:T(8,128)} collective-permute-done((f32[64,768]{1,0:T(8,128)S(1)}, f32[64,768]{1,0:T(8,128)}, u32[]{:S(2)}, u32[]{:S(2)}) %collective-permute-start.3) | collective-permute-done | bytes 196640 | tf_op jit(solution)/shard_map/ppermute | solution.py:12
  120.0 2.4 fusion.15
  122.4 0.0 all-reduce.11.cloned.1.call-update
  122.4 0.0 all-reduce.13.cloned.1.call-start
  122.5 2.1 fusion.34
  124.6 31.4 %all-reduce.11.cloned.1.call-done = f32[64,768]{1,0:T(8,128)} async-done(((f32[64,768]{1,0:T(8,128)}), f32[64,768]{1,0:T(8,128)}) %all-reduce.11.cloned.1.call-update) | async-done | bytes 196624 | tf_op jit(solution)/shard_map/psum | solution.py:28
  156.0 2.8 %fusion.35 = f32[64,768]{1,0:T(8,128)} fusion(f32[64,768]{1,0:T(8,128)S(1)} %fusion.34, bf16[768,24]{1,0:T(8,128)(2,1)S(1)} %copy-done.6, bf16[3,768,768]{2,1,0:T(8,128)(2,1)} %param.14, s32[768]{0:T(1024)S(1)} %copy-done.11, f32[64,768]{1,0:T(8,128)} %all-reduce.11.cloned.1.call-done), kind=kOutput, calls=%fused_computation.41 | convolution fusion | flops 104515584 | bytes 1809408 | tf_op jit(solution)/shard_map/dot_general | solution.py:69
  158.9 0.0 all-reduce.13.cloned.1.call-update
  158.9 0.0 all-reduce.15.cloned.1.call-start
  158.9 35.1 %all-reduce.13.cloned.1.call-done = f32[64,768]{1,0:T(8,128)} async-done(((f32[64,768]{1,0:T(8,128)}), f32[64,768]{1,0:T(8,128)}) %all-reduce.13.cloned.1.call-update) | async-done | bytes 196624 | tf_op jit(solution)/shard_map/psum | solution.py:72
  194.0 0.0 all-reduce.15.cloned.1.call-update
  194.1 0.0 all-reduce.17.cloned.1.call-start
  194.1 24.1 %all-reduce.15.cloned.1.call-done = f32[64,768]{1,0:T(8,128)} async-done(((f32[64,768]{1,0:T(8,128)}), f32[64,768]{1,0:T(8,128)}) %all-reduce.15.cloned.1.call-update) | async-done | bytes 196624 | tf_op jit(solution)/shard_map/psum | solution.py:73
  218.3 2.2 fusion.62
  220.5 0.0 all-reduce.17.cloned.1.call-update
  220.5 0.9 pad_maximum_fusion
  221.4 32.5 %all-reduce.17.cloned.1.call-done = f32[64,1536]{1,0:T(8,128)} async-done(((f32[64,1536]{1,0:T(8,128)}), f32[64,1536]{1,0:T(8,128)}) %all-reduce.17.cloned.1.call-update) | async-done | bytes 393232 | tf_op jit(solution)/shard_map/psum | solution.py:28
  253.9 1.8 copy.16
  (24 shorter events, 0.1 us)
Async XLA Ops:
  7.2 211.1 %copy-start = (bf16[768,1536]{1,0:T(8,128)(2,1)S(1)}, bf16[768,1536]{1,0:T(8,128)(2,1)}, u32[]{:S(2)}) copy-start(bf16[768,1536]{1,0:T(8,128)(2,1)} %param.11) | copy-start | bytes 7077892
  7.2 2.7 %copy-start.8 = (s32[3,6,24]{2,1,0:T(8,128)S(1)}, s32[3,6,24]{2,1,0:T(8,128)}, u32[]{:S(2)}) copy-start(s32[3,6,24]{2,1,0:T(8,128)} %param.13) | copy-start | bytes 5188
  7.2 38.5 %all-reduce.7.cloned.1.call-start = ((), (), s32[]{:S(2)}) async-start(), calls=%async_computation | async-start | bytes 393216 | tf_op jit(solution)/shard_map/psum | solution.py:28
  9.8 89.0 %all-reduce.9.cloned.1.call-start = ((), (), s32[]{:S(2)}) async-start(), calls=%async_computation.1 | async-start | bytes 393216 | tf_op jit(solution)/shard_map/psum | solution.py:28
  11.0 51.9 %copy-start.1 = (f32[1,3,64,768]{3,2,1,0:T(8,128)S(1)}, f32[1,3,64,768]{3,2,1,0:T(8,128)}, u32[]{:S(2)}) copy-start(f32[1,3,64,768]{3,2,1,0:T(8,128)} %param.8) | copy-start | bytes 1769476
  47.8 5.7 %collective-permute-start = (f32[64,768]{1,0:T(8,128)S(1)}, f32[64,768]{1,0:T(8,128)S(1)}, u32[]{:S(2)}, u32[]{:S(2)}) collective-permute-start(f32[64,768]{1,0:T(8,128)S(1)} %fusion.11), channel_id=1, source_target_pairs={{0,1},{1,0},{2,3},{3,2},{4,5},{5,4},{6,7},{7,6},{8,9},{9,8},{10,11... | collective-permute-start | bytes 589832 | tf_op jit(solution)/shard_map/ppermute | solution.py:12
  53.6 11.7 %copy-start.9 = (s32[3,6,24]{2,1,0:T(8,128)S(1)}, s32[3,6,24]{2,1,0:T(8,128)}, u32[]{:S(2)}) copy-start(s32[3,6,24]{2,1,0:T(8,128)} %param.15) | copy-start | bytes 5188
  53.6 9.4 %collective-permute-start.1 = (f32[64,768]{1,0:T(8,128)S(1)}, f32[64,768]{1,0:T(8,128)S(1)}, u32[]{:S(2)}, u32[]{:S(2)}) collective-permute-start(f32[64,768]{1,0:T(8,128)S(1)} %add.60), channel_id=1, source_target_pairs={{0,2},{1,3},{2,0},{3,1},{4,6},{5,7},{6,4},{7,5},{8,10},{9,11},{10,... | collective-permute-start | bytes 589832 | tf_op jit(solution)/shard_map/ppermute | solution.py:12
  57.7 41.1 %copy-start.10 = (s32[768]{0:T(1024)S(1)}, s32[768]{0:T(1024)}, u32[]{:S(2)}) copy-start(s32[768]{0:T(1024)} %add_select_fusion) | copy-start | bytes 9220
  65.2 36.4 %copy-start.3 = (f32[64,768]{1,0:T(8,128)S(1)}, f32[64,768]{1,0:T(8,128)}, u32[]{:S(2)}) copy-start(f32[64,768]{1,0:T(8,128)} %all-reduce.7.cloned.1.call-done) | copy-start | bytes 589828
  65.2 90.8 %all-reduce.11.cloned.1.call-start = ((), (), s32[]{:S(2)}) async-start(), calls=%async_computation.2 | async-start | bytes 393216 | tf_op jit(solution)/shard_map/psum | solution.py:28
  101.7 11.4 %copy-start.4 = (f32[64,768]{1,0:T(8,128)S(1)}, f32[64,768]{1,0:T(8,128)}, u32[]{:S(2)}) copy-start(f32[64,768]{1,0:T(8,128)} %all-reduce.9.cloned.1.call-done) | copy-start | bytes 589828
  103.9 2.5 copy-start.7
  103.9 5.7 %collective-permute-start.2 = (f32[64,768]{1,0:T(8,128)S(1)}, f32[64,768]{1,0:T(8,128)S(1)}, u32[]{:S(2)}, u32[]{:S(2)}) collective-permute-start(f32[64,768]{1,0:T(8,128)S(1)} %fusion.33), channel_id=1, source_target_pairs={{0,1},{1,0},{2,3},{3,2},{4,5},{5,4},{6,7},{7,6},{8,9},{9,8},{10,11... | collective-permute-start | bytes 589832 | tf_op jit(solution)/shard_map/ppermute | solution.py:12
  110.6 9.5 %collective-permute-start.3 = (f32[64,768]{1,0:T(8,128)S(1)}, f32[64,768]{1,0:T(8,128)}, u32[]{:S(2)}, u32[]{:S(2)}) collective-permute-start(f32[64,768]{1,0:T(8,128)S(1)} %add.63), channel_id=1, source_target_pairs={{0,2},{1,3},{2,0},{3,1},{4,6},{5,7},{6,4},{7,5},{8,10},{9,11},{10,... | collective-permute-start | bytes 589832 | tf_op jit(solution)/shard_map/ppermute | solution.py:12
  115.9 6.6 %copy-start.11 = (s32[768]{0:T(1024)S(1)}, s32[768]{0:T(1024)}, u32[]{:S(2)}) copy-start(s32[768]{0:T(1024)} %add_select_fusion) | copy-start | bytes 9220
  122.4 33.6 %copy-start.6 = (bf16[768,24]{1,0:T(8,128)(2,1)S(1)}, bf16[768,24]{1,0:T(8,128)(2,1)}, u32[]{:S(2)}) copy-start(bf16[768,24]{1,0:T(8,128)(2,1)} %fusion.36) | copy-start | bytes 110596
  122.4 71.6 %all-reduce.13.cloned.1.call-start = ((), (), s32[]{:S(2)}) async-start(), calls=%async_computation.3 | async-start | bytes 393216 | tf_op jit(solution)/shard_map/psum | solution.py:72
  124.6 93.6 %copy-start.2 = (f32[64,768]{1,0:T(8,128)S(1)}, f32[64,768]{1,0:T(8,128)}, u32[]{:S(2)}) copy-start(f32[64,768]{1,0:T(8,128)} %param.9) | copy-start | bytes 589828
  158.9 59.4 %all-reduce.15.cloned.1.call-start = ((), (), s32[]{:S(2)}) async-start(), calls=%async_computation.4 | async-start | bytes 393216 | tf_op jit(solution)/shard_map/psum | solution.py:73
  194.1 26.4 %copy-start.5 = (f32[64,768]{1,0:T(8,128)S(1)}, f32[64,768]{1,0:T(8,128)}, u32[]{:S(2)}) copy-start(f32[64,768]{1,0:T(8,128)} %all-reduce.11.cloned.1.call-done) | copy-start | bytes 589828
  194.1 59.8 %all-reduce.17.cloned.1.call-start = ((), (), s32[]{:S(2)}) async-start(), calls=%async_computation.5 | async-start | bytes 786432 | tf_op jit(solution)/shard_map/psum | solution.py:28
Sparse Core Ops, SparseCore 0:
  10.9 34.7 all-reduce.6
  65.3 33.4 all-reduce.8
  122.6 33.4 all-reduce.10
  159.0 34.9 all-reduce.12
  196.2 22.0 all-reduce.14
  221.1 32.7 all-reduce.16
where the time goes:
time: 263 us
  waiting for transfers between devices  206 us (78%)
  matrix products  29.5 us (11%)
  between operations  14.3 us (5%)
  starting transfers between devices  8.29 us (3%)
    psum x4, waiting for transfers between devices, solve_block(): return lax.psum(partial_sum, 'prow')  131 us
    psum x1, waiting for transfers between devices, shards(): across = lax.psum(root_local, 'pcol')  35.1 us
    psum x1, waiting for transfers between devices, shards(): root_update = lax.psum(across, 'grid')  24.1 us
    ppermute x4, waiting for transfers between devices, from_partner(): lax.ppermute(shard, axis, [(i, i ^ 1 << bit) for i in range(lax.axis_size...  15.8 us
    dot_general x6, matrix products, shards(): jnp.dot(kept[source], factor_tile, preferred_element_type=jnp.float32)  14.9 us
    dot_general x4, matrix products, solve_block(): jnp.dot(residual.astype(jnp.bfloat16), inverse, preferred_element_type=jn...  9.38 us
    ppermute x4, starting transfers between devices, from_partner(): lax.ppermute(shard, axis, [(i, i ^ 1 << bit) for i in range(lax.axis_size...  8.05 us
  transfers between devices with their start and end apart: 10, of which 10 were waited for; matrix products, arithmetic and copies ran while one was open for 4% of the time, Pallas kernels for 0%

commit v1 on v0

--- a/solution.py
+++ b/solution.py
@@ -69,7 +69,7 @@
         root_local = root_local + jnp.dot(
             kept[source], factor_tile, preferred_element_type=jnp.float32
         )
-    across = lax.psum(root_local, "pcol")
+    across = jnp.sum(lax.all_gather(root_local, axis_name="pcol"), 0)
     root_update = lax.psum(across, "grid")
     root_solution = solve_block(root_rhs - root_update, root_inverse)
     return (jnp.stack(solved_all), root_solution)

time: 263 us -> 245 us (0.932)
  waiting for transfers between devices: 206 us -> 168 us
  blocking collectives: 0 us -> 19.8 us
    psum x1 -> x0, waiting for transfers between devices: 35.1 us -> none  [shards(): across = lax.psum(root_local, 'pcol')]
    all_gather x0 -> x1, blocking collectives: none -> 19.8 us  [shards(): across = jnp.sum(lax.all_gather(root_local, axis_name='pcol'), 0)]
    psum x1, waiting for transfers between devices: 24.1 us -> 21 us  [shards(): root_update = lax.psum(across, 'grid')]
  transfers between devices with their start and end apart: 10 -> 9, of which waited for: 10 -> 9; matrix products, arithmetic and copies ran while one was open for 4% -> 5% of each run, Pallas kernels for 0% -> 0%
where the time goes in v1:
time: 245 us; the launch traced here: 244 us
  waiting for transfers between devices  168 us (69%)
  matrix products  29.4 us (12%)
  blocking collectives  19.8 us (8%)
  between operations  13.9 us (6%)
  starting transfers between devices  8.25 us (3%)
  other arithmetic  3.16 us (1%)
    psum x4, waiting for transfers between devices, solve_block(): return lax.psum(partial_sum, 'prow')  131 us
    psum x1, waiting for transfers between devices, shards(): root_update = lax.psum(across, 'grid')  21 us
    all_gather x1, blocking collectives, shards(): across = jnp.sum(lax.all_gather(root_local, axis_name='pcol'), 0)  19.8 us
    ppermute x4, waiting for transfers between devices, from_partner(): lax.ppermute(shard, axis, [(i, i ^ 1 << bit) for i in range(lax.axis_size...  15.8 us
    dot_general x6, matrix products, shards(): jnp.dot(kept[source], factor_tile, preferred_element_type=jnp.float32)  14.9 us
    dot_general x4, matrix products, solve_block(): jnp.dot(residual.astype(jnp.bfloat16), inverse, preferred_element_type=jn...  9.39 us
    ppermute x4, starting transfers between devices, from_partner(): lax.ppermute(shard, axis, [(i, i ^ 1 << bit) for i in range(lax.axis_size...  8.05 us
    dot_general x6, matrix products, masked(): jnp.dot(row_select, mask.astype(jnp.float32))  5.13 us
  transfers between devices with their start and end apart: 9, of which 9 were waited for; matrix products, arithmetic and copies ran while one was open for 5% of the time, Pallas kernels for 0%

profile of v1, /device:TPU:0, one launch (start us, length us, event | category | flops | bytes accessed | tf_op | source)
XLA Modules:
  0.0 244.3 jit_solution(17635210643345866741)
XLA Ops:
  7.2 0.0 copy-start
  7.2 0.0 all-reduce.6.cloned.1.call-start
  7.2 2.5 %fusion.22 = f32[64,768]{1,0:T(8,128)} fusion(bf16[3,768,768]{2,1,0:T(8,128)(2,1)} %param.10, f32[1,3,64,768]{3,2,1,0:T(8,128)} %param.8), kind=kOutput, calls=%fused_computation.28 | convolution fusion | flops 75497472 | bytes 1474560 | tf_op jit(solution)/shard_map/dot_general | solution.py:25
  9.8 0.0 all-reduce.6.cloned.1.call-update
  9.8 0.0 all-reduce.8.cloned.1.call-start
  9.9 0.3 fusion.41
  10.2 0.3 fusion.39
  10.4 0.6 add_select_fusion
  11.1 34.6 %all-reduce.6.cloned.1.call-done = f32[64,768]{1,0:T(8,128)} async-done(((f32[64,768]{1,0:T(8,128)}), f32[64,768]{1,0:T(8,128)}) %all-reduce.6.cloned.1.call-update) | async-done | bytes 196624 | tf_op jit(solution)/shard_map/psum | solution.py:28
  45.7 2.1 fusion.11
  47.8 1.6 collective-permute-start
  49.4 1.0 fusion.40
  50.3 3.2 %collective-permute-done = f32[64,768]{1,0:T(8,128)S(1)} collective-permute-done((f32[64,768]{1,0:T(8,128)S(1)}, f32[64,768]{1,0:T(8,128)S(1)}, u32[]{:S(2)}, u32[]{:S(2)}) %collective-permute-start) | collective-permute-done | bytes 196640 | tf_op jit(solution)/shard_map/ppermute | solution.py:12
  53.6 0.0 copy-start.11
  53.6 2.5 %collective-permute-start.1 = (f32[64,768]{1,0:T(8,128)S(1)}, f32[64,768]{1,0:T(8,128)S(1)}, u32[]{:S(2)}, u32[]{:S(2)}) collective-permute-start(f32[64,768]{1,0:T(8,128)S(1)} %add.58), channel_id=1, source_target_pairs={{0,2},{1,3},{2,0},{3,1},{4,6},{5,7},{6,4},{7,5},{8,10},{9,11},{10,... | collective-permute-start | bytes 589832 | tf_op jit(solution)/shard_map/ppermute | solution.py:12
  56.0 1.7 fusion.37
  57.7 5.2 %collective-permute-done.1 = f32[64,768]{1,0:T(8,128)S(1)} collective-permute-done((f32[64,768]{1,0:T(8,128)S(1)}, f32[64,768]{1,0:T(8,128)S(1)}, u32[]{:S(2)}, u32[]{:S(2)}) %collective-permute-start.1) | collective-permute-done | bytes 196640 | tf_op jit(solution)/shard_map/ppermute | solution.py:12
  62.9 2.3 fusion.19
  65.2 0.0 all-reduce.8.cloned.1.call-update
  65.2 0.0 all-reduce.10.cloned.1.call-start
  65.3 1.0 fusion.38
  66.3 32.6 %all-reduce.8.cloned.1.call-done = f32[64,768]{1,0:T(8,128)} async-done(((f32[64,768]{1,0:T(8,128)}), f32[64,768]{1,0:T(8,128)}) %all-reduce.8.cloned.1.call-update) | async-done | bytes 196624 | tf_op jit(solution)/shard_map/psum | solution.py:28
  98.8 2.8 %fusion.9 = f32[64,768]{1,0:T(8,128)} fusion(bf16[768,24]{1,0:T(8,128)(2,1)S(1)} %fusion.39, bf16[3,768,768]{2,1,0:T(8,128)(2,1)} %param.12, s32[768]{0:T(1024)S(1)} %copy-done.12, f32[64,768]{1,0:T(8,128)} %all-reduce.8.cloned.1.call-done), kind=kOutput, calls=%fused_computation.15 | convolution fusion | flops 104466432 | bytes 1612800 | tf_op jit(solution)/shard_map/dot_general | solution.py:58
  101.7 2.2 fusion.33
  103.9 0.0 copy-start.9
  103.9 1.6 collective-permute-start.2
  105.4 1.0 fusion.36
  106.4 3.2 %collective-permute-done.2 = f32[64,768]{1,0:T(8,128)S(1)} collective-permute-done((f32[64,768]{1,0:T(8,128)S(1)}, f32[64,768]{1,0:T(8,128)S(1)}, u32[]{:S(2)}, u32[]{:S(2)}) %collective-permute-start.2) | collective-permute-done | bytes 196640 | tf_op jit(solution)/shard_map/ppermute | solution.py:12
  109.6 1.0 add.61
  110.6 2.5 %collective-permute-start.3 = (f32[64,768]{1,0:T(8,128)S(1)}, f32[64,768]{1,0:T(8,128)}, u32[]{:S(2)}, u32[]{:S(2)}) collective-permute-start(f32[64,768]{1,0:T(8,128)S(1)} %add.61), channel_id=1, source_target_pairs={{0,2},{1,3},{2,0},{3,1},{4,6},{5,7},{6,4},{7,5},{8,10},{9,11},{10,... | collective-permute-start | bytes 589832 | tf_op jit(solution)/shard_map/ppermute | solution.py:12
  113.0 2.8 %fusion.7 = f32[64,768]{1,0:T(8,128)} fusion(bf16[768,24]{1,0:T(8,128)(2,1)} %fusion.37, bf16[3,768,768]{2,1,0:T(8,128)(2,1)} %param.14, s32[768]{0:T(1024)} %add_select_fusion, f32[64,768]{1,0:T(8,128)S(1)} %copy-done.4), kind=kOutput, calls=%fused_computation.13 | convolution fusion | flops 104466432 | bytes 1773568 | tf_op jit(solution)/shard_map/dot_general | solution.py:69
  115.9 4.1 %collective-permute-done.3 = f32[64,768]{1,0:T(8,128)} collective-permute-done((f32[64,768]{1,0:T(8,128)S(1)}, f32[64,768]{1,0:T(8,128)}, u32[]{:S(2)}, u32[]{:S(2)}) %collective-permute-start.3) | collective-permute-done | bytes 196640 | tf_op jit(solution)/shard_map/ppermute | solution.py:12
  120.0 2.4 fusion.15
  122.4 0.0 all-reduce.10.cloned.1.call-update
  122.4 0.0 all-reduce.12.cloned.1.call-start
  122.5 2.0 fusion.34
  124.6 31.5 %all-reduce.10.cloned.1.call-done = f32[64,768]{1,0:T(8,128)} async-done(((f32[64,768]{1,0:T(8,128)}), f32[64,768]{1,0:T(8,128)}) %all-reduce.10.cloned.1.call-update) | async-done | bytes 196624 | tf_op jit(solution)/shard_map/psum | solution.py:28
  156.0 2.8 %fusion.35 = f32[64,768]{1,0:T(8,128)} fusion(f32[64,768]{1,0:T(8,128)S(1)} %fusion.34, bf16[768,24]{1,0:T(8,128)(2,1)S(1)} %copy-done.8, bf16[3,768,768]{2,1,0:T(8,128)(2,1)} %param.14, s32[768]{0:T(1024)S(1)} %copy-done.13, f32[64,768]{1,0:T(8,128)} %all-reduce.10.cloned.1.call-done), kind=kOutput, calls=%fused_computation.41 | convolution fusion | flops 104515584 | bytes 1809408 | tf_op jit(solution)/shard_map/dot_general | solution.py:69
  158.9 19.8 %all-gather = f32[256,768]{1,0:T(8,128)S(1)} all-gather(f32[64,768]{1,0:T(8,128)} %fusion.35), channel_id=2, replica_groups=mesh['grid'=2,'prow'=4,'pcol'=4] {'pcol'}, dimensions={0}, use_global_device_ids=true | all-gather | bytes 983040 | tf_op jit(solution)/shard_map/all_gather | solution.py:72
  178.6 0.7 reduce_sum.9
  179.4 0.0 all-reduce.12.cloned.1.call-update
  179.4 0.0 all-reduce.14.cloned.1.call-start
  179.5 21.0 %all-reduce.12.cloned.1.call-done = f32[64,768]{1,0:T(8,128)} async-done(((f32[64,768]{1,0:T(8,128)}), f32[64,768]{1,0:T(8,128)}) %all-reduce.12.cloned.1.call-update) | async-done | bytes 196624 | tf_op jit(solution)/shard_map/psum | solution.py:73
  200.4 2.2 fusion.62
  202.6 0.0 all-reduce.14.cloned.1.call-update
  202.7 0.9 pad_maximum_fusion
  203.5 32.5 %all-reduce.14.cloned.1.call-done = f32[64,1536]{1,0:T(8,128)} async-done(((f32[64,1536]{1,0:T(8,128)}), f32[64,1536]{1,0:T(8,128)}) %all-reduce.14.cloned.1.call-update) | async-done | bytes 393232 | tf_op jit(solution)/shard_map/psum | solution.py:28
  236.0 1.8 copy.15
  (27 shorter events, 0.1 us)
Async XLA Ops:
  7.2 193.2 %copy-start = (bf16[768,1536]{1,0:T(8,128)(2,1)S(1)}, bf16[768,1536]{1,0:T(8,128)(2,1)}, u32[]{:S(2)}) copy-start(bf16[768,1536]{1,0:T(8,128)(2,1)} %param.11) | copy-start | bytes 7077892
  7.2 2.7 %copy-start.10 = (s32[3,6,24]{2,1,0:T(8,128)S(1)}, s32[3,6,24]{2,1,0:T(8,128)}, u32[]{:S(2)}) copy-start(s32[3,6,24]{2,1,0:T(8,128)} %param.13) | copy-start | bytes 5188
  7.2 38.5 %all-reduce.6.cloned.1.call-start = ((), (), s32[]{:S(2)}) async-start(), calls=%async_computation | async-start | bytes 393216 | tf_op jit(solution)/shard_map/psum | solution.py:28
  9.8 89.0 %all-reduce.8.cloned.1.call-start = ((), (), s32[]{:S(2)}) async-start(), calls=%async_computation.1 | async-start | bytes 393216 | tf_op jit(solution)/shard_map/psum | solution.py:28
  11.1 51.9 %copy-start.1 = (f32[1,3,64,768]{3,2,1,0:T(8,128)S(1)}, f32[1,3,64,768]{3,2,1,0:T(8,128)}, u32[]{:S(2)}) copy-start(f32[1,3,64,768]{3,2,1,0:T(8,128)} %param.8) | copy-start | bytes 1769476
  47.8 5.7 %collective-permute-start = (f32[64,768]{1,0:T(8,128)S(1)}, f32[64,768]{1,0:T(8,128)S(1)}, u32[]{:S(2)}, u32[]{:S(2)}) collective-permute-start(f32[64,768]{1,0:T(8,128)S(1)} %fusion.11), channel_id=1, source_target_pairs={{0,1},{1,0},{2,3},{3,2},{4,5},{5,4},{6,7},{7,6},{8,9},{9,8},{10,11... | collective-permute-start | bytes 589832 | tf_op jit(solution)/shard_map/ppermute | solution.py:12
  53.6 11.7 %copy-start.11 = (s32[3,6,24]{2,1,0:T(8,128)S(1)}, s32[3,6,24]{2,1,0:T(8,128)}, u32[]{:S(2)}) copy-start(s32[3,6,24]{2,1,0:T(8,128)} %param.15) | copy-start | bytes 5188
  53.6 9.4 %collective-permute-start.1 = (f32[64,768]{1,0:T(8,128)S(1)}, f32[64,768]{1,0:T(8,128)S(1)}, u32[]{:S(2)}, u32[]{:S(2)}) collective-permute-start(f32[64,768]{1,0:T(8,128)S(1)} %add.58), channel_id=1, source_target_pairs={{0,2},{1,3},{2,0},{3,1},{4,6},{5,7},{6,4},{7,5},{8,10},{9,11},{10,... | collective-permute-start | bytes 589832 | tf_op jit(solution)/shard_map/ppermute | solution.py:12
  57.7 41.1 %copy-start.12 = (s32[768]{0:T(1024)S(1)}, s32[768]{0:T(1024)}, u32[]{:S(2)}) copy-start(s32[768]{0:T(1024)} %add_select_fusion) | copy-start | bytes 9220
  65.2 36.4 %copy-start.3 = (f32[64,768]{1,0:T(8,128)S(1)}, f32[64,768]{1,0:T(8,128)}, u32[]{:S(2)}) copy-start(f32[64,768]{1,0:T(8,128)} %all-reduce.6.cloned.1.call-done) | copy-start | bytes 589828
  65.2 90.8 %all-reduce.10.cloned.1.call-start = ((), (), s32[]{:S(2)}) async-start(), calls=%async_computation.2 | async-start | bytes 393216 | tf_op jit(solution)/shard_map/psum | solution.py:28
  101.7 11.4 %copy-start.4 = (f32[64,768]{1,0:T(8,128)S(1)}, f32[64,768]{1,0:T(8,128)}, u32[]{:S(2)}) copy-start(f32[64,768]{1,0:T(8,128)} %all-reduce.8.cloned.1.call-done) | copy-start | bytes 589828
  103.9 2.5 %copy-start.9 = (f32[64,768]{1,0:T(8,128)}, f32[64,768]{1,0:T(8,128)S(1)}, u32[]{:S(2)}) copy-start(f32[64,768]{1,0:T(8,128)S(1)} %fusion.33) | copy-start | bytes 589828
  103.9 5.7 %collective-permute-start.2 = (f32[64,768]{1,0:T(8,128)S(1)}, f32[64,768]{1,0:T(8,128)S(1)}, u32[]{:S(2)}, u32[]{:S(2)}) collective-permute-start(f32[64,768]{1,0:T(8,128)S(1)} %fusion.33), channel_id=1, source_target_pairs={{0,1},{1,0},{2,3},{3,2},{4,5},{5,4},{6,7},{7,6},{8,9},{9,8},{10,11... | collective-permute-start | bytes 589832 | tf_op jit(solution)/shard_map/ppermute | solution.py:12
  110.6 9.5 %collective-permute-start.3 = (f32[64,768]{1,0:T(8,128)S(1)}, f32[64,768]{1,0:T(8,128)}, u32[]{:S(2)}, u32[]{:S(2)}) collective-permute-start(f32[64,768]{1,0:T(8,128)S(1)} %add.61), channel_id=1, source_target_pairs={{0,2},{1,3},{2,0},{3,1},{4,6},{5,7},{6,4},{7,5},{8,10},{9,11},{10,... | collective-permute-start | bytes 589832 | tf_op jit(solution)/shard_map/ppermute | solution.py:12
  115.9 6.6 %copy-start.7 = (bf16[768,24]{1,0:T(8,128)(2,1)S(1)}, bf16[768,24]{1,0:T(8,128)(2,1)}, u32[]{:S(2)}) copy-start(bf16[768,24]{1,0:T(8,128)(2,1)} %fusion.38) | copy-start | bytes 110596
  115.9 6.6 %copy-start.13 = (s32[768]{0:T(1024)S(1)}, s32[768]{0:T(1024)}, u32[]{:S(2)}) copy-start(s32[768]{0:T(1024)} %add_select_fusion) | copy-start | bytes 9220
  122.4 33.6 %copy-start.8 = (bf16[768,24]{1,0:T(8,128)(2,1)S(1)}, bf16[768,24]{1,0:T(8,128)(2,1)}, u32[]{:S(2)}) copy-start(bf16[768,24]{1,0:T(8,128)(2,1)} %fusion.36) | copy-start | bytes 110596
  122.4 78.0 %all-reduce.12.cloned.1.call-start = ((), (), s32[]{:S(2)}) async-start(), calls=%async_computation.3 | async-start | bytes 393216 | tf_op jit(solution)/shard_map/psum | solution.py:73
  158.9 41.5 %copy-start.2 = (f32[64,768]{1,0:T(8,128)S(1)}, f32[64,768]{1,0:T(8,128)}, u32[]{:S(2)}) copy-start(f32[64,768]{1,0:T(8,128)} %param.9) | copy-start | bytes 589828
  179.4 23.3 %copy-start.5 = (f32[64,768]{1,0:T(8,128)S(1)}, f32[64,768]{1,0:T(8,128)}, u32[]{:S(2)}) copy-start(f32[64,768]{1,0:T(8,128)} %all-reduce.8.cloned.1.call-done) | copy-start | bytes 589828
  179.4 23.3 %copy-start.6 = (f32[64,768]{1,0:T(8,128)S(1)}, f32[64,768]{1,0:T(8,128)}, u32[]{:S(2)}) copy-start(f32[64,768]{1,0:T(8,128)} %all-reduce.10.cloned.1.call-done) | copy-start | bytes 589828
  179.4 56.6 %all-reduce.14.cloned.1.call-start = ((), (), s32[]{:S(2)}) async-start(), calls=%async_computation.4 | async-start | bytes 786432 | tf_op jit(solution)/shard_map/psum | solution.py:28
Sparse Core Ops, SparseCore 0:
  10.9 34.7 all-reduce.5
  65.3 33.4 all-reduce.7
  122.6 33.4 all-reduce.9
  179.5 20.8 all-reduce.11
  203.2 32.7 all-reduce.13
